TPU v7x, 128 devices: a whole 4x4x4 slice. The times are simulated.
128 devices in a mesh: seg: 32 (over y, z, core), grp: 4 (over x).
Axes of the slice: x: 4, y: 4, z: 4, core: 2. Of those that a mesh axis runs over, the one named last changes fastest.
Arguments:
- basis: float32 [8, 3072, 128], P(None, ('seg', 'grp')), may hold values from -6 to 6
- coords: float32 [3072, 3, 128], P(('seg', 'grp')), may hold values from 0 to 4
- areas: float32 [3072, 128], P(('seg', 'grp')), may hold values from 0.5 to 2
- p2m: bfloat16 [3072, 121, 128], P(('seg', 'grp')), may hold values from -0.5 to 0.5
- l2p: bfloat16 [3072, 128, 121], P(('seg', 'grp')), may hold values from -0.5 to 0.5
- m2l: bfloat16 [316, 121, 121], replicated, may hold values from -0.0390625 to 0.0390625
- counts: int32 [128], P(('seg', 'grp')), may hold values from 8 to 24
- near_list: int32 [3072, 27], P(('seg', 'grp')), may hold values from 0 to 287
- far_list: int32 [3072, 189], P(('seg', 'grp')), may hold values from 0 to 287
- far_offset: int32 [3072, 189], P(('seg', 'grp')), may hold values from 0 to 315
Outputs:
- new_vector: float32 [3072, 128], P(('seg', 'grp'))
- hessenberg: float32 [9], replicated
Inputs may be any that keep to these rules, and one draw needn't show every extreme that they name: `near_list`: window indices follow the rule of the steps; entries may name empty slots or leaves beyond the ends of the curve, which contribute nothing. A device's live leaves are its first counts slots.
All inputs are finite; a program needn't handle non-finite values.
Results may differ from a plain program's by a relative error of at most 0.0012.
Values sent between devices are 32-bit elements; how exact they have to be, the bound alone decides.
A program may use at most 64 MiB of HBM per device.

v0:
```python
import math
import jax
import jax.numpy as jnp
from jax import lax
from jax.sharding import Mesh
from jax.sharding import PartitionSpec as P

SEG = ("seg_0", "seg_1", "seg_2")
SEG_GRP = ("seg_0", "seg_1", "seg_2", "grp")
four_pi = 12.566370614359172
epsilon = 1e-06
highest = lax.Precision.HIGHEST


def from_everyone(value, axis):
    copies = jnp.broadcast_to(value, (lax.axis_size(axis), *value.shape))
    return lax.all_to_all(copies, axis, split_axis=0, concat_axis=0, tiled=True)


def in_order(pieces, dim):
    lengths = list(pieces.shape[1:])
    lengths[dim] *= pieces.shape[0]
    return jnp.moveaxis(pieces, 0, dim).reshape(lengths)


def gathered_copies(value, axis, dim):
    pieces = from_everyone(value, axis)
    return in_order(pieces, dim)


def in_one_piece(arrays, axis, dim, along):
    widths = [math.prod(a.shape[along:]) for a in arrays]
    both = jnp.concatenate(
        [a.reshape(*a.shape[:along], w) for a, w in zip(arrays, widths)], axis=along
    )
    whole = gathered_copies(both, axis, dim)
    pieces = jnp.split(whole, [sum(widths[:k]) for k in range(1, len(widths))], axis=along)
    return tuple(
        (b.reshape(*whole.shape[:along], *a.shape[along:]) for a, b in zip(arrays, pieces))
    )


def with_halo(cells, sides, width):
    for axis, dim in sides:
        count = lax.axis_size(axis)
        ends = count - 1
        head = lax.slice_in_dim(cells, 0, width, axis=dim)
        tail = lax.slice_in_dim(cells, cells.shape[dim] - width, cells.shape[dim], axis=dim)
        cells = jnp.concatenate(
            [
                lax.ppermute(tail, axis, [(i, (i + 1) % count) for i in range(ends)]),
                cells,
                lax.ppermute(head, axis, [((i + 1) % count, i) for i in range(ends)]),
            ],
            axis=dim,
        )
    return cells


def by_axis(value, axes):
    for axis in axes:
        value = lax.psum(value, axis)
    return value


def near_field(coords, wide_panels, near_list):
    leaf_count = coords.shape[0]
    panels = coords.shape[2]

    def near_step(running, column):
        source = jnp.take(wide_panels, column, axis=0)
        square = jnp.zeros((leaf_count, panels, panels), jnp.float32)
        for component in range(3):
            spread = coords[:, component, :, None] - source[:, component, None, :]
            square = square + spread * spread
        source_area = source[:, 3, None, :]
        kernel = source_area / (four_pi * jnp.sqrt(square + source_area))
        return (running + jnp.sum(kernel * source[:, 4, None, :], axis=2), None)

    result, _ = lax.scan(near_step, jnp.zeros((leaf_count, panels), jnp.float32), near_list.T)
    return result


def far_field(wide_poles, m2l, far_list, far_offset):
    offsets = m2l.shape[0]
    gathered = jnp.take(wide_poles, far_list, axis=0)
    offset_hot = (
        far_offset[:, :, None] == lax.broadcasted_iota(jnp.int32, (1, 1, offsets), 2)
    ).astype(jnp.float32)
    summed = jnp.einsum("tfo,tfk->tok", offset_hot, gathered, precision=highest)
    return jnp.einsum("tok,oik->ti", summed, m2l.astype(jnp.float32), precision=highest)


def on_device(basis, coords, areas, p2m, l2p, m2l, counts, near_list, far_list, far_offset):
    leaf_count, panels = areas.shape
    krylov = basis.shape[0]
    slots = lax.broadcasted_iota(jnp.int32, (leaf_count, 1), 0)
    live_mask = (slots < counts[0]).astype(jnp.float32)
    current = basis[krylov - 1] * live_mask
    rounded = current.astype(jnp.bfloat16)
    multipoles = jnp.einsum("lkp,lp->lk", p2m, rounded, preferred_element_type=jnp.float32)
    packed = jnp.concatenate([coords, areas[:, None, :], current[:, None, :]], axis=1)
    group_panels, group_poles = in_one_piece((packed, multipoles), "grp", 0, 1)
    wide_panels, wide_poles = (
        with_halo(group_panels, ((SEG, 0),), group_panels.shape[0]),
        with_halo(group_poles, ((SEG, 0),), group_panels.shape[0]),
    )
    nearby = near_field(coords, wide_panels, near_list)
    local = far_field(wide_poles, m2l, far_list, far_offset).astype(jnp.bfloat16)
    distant = jnp.einsum("lpk,lk->lp", l2p, local, preferred_element_type=jnp.float32)
    image = (0.5 * current + nearby + distant) * live_mask
    masked = basis * live_mask[None]
    products = jnp.einsum("jlp,lp->j", masked, image, precision=highest)
    live_panels = jnp.sum(live_mask) * panels
    gram = jnp.einsum("ilp,jlp->ij", masked, masked, precision=highest)
    summed, population, gram_sum, energy = (
        by_axis(products, SEG_GRP),
        by_axis(live_panels, SEG_GRP),
        by_axis(gram, SEG_GRP),
        by_axis(jnp.sum(image * image), SEG_GRP),
    )
    coefficients = summed / population
    residue = image - jnp.einsum("j,jlp->lp", coefficients, masked, precision=highest)
    curvature = jnp.dot(
        coefficients, jnp.dot(gram_sum, coefficients, precision=highest), precision=highest
    )
    squares = energy - 2.0 * jnp.dot(coefficients, summed, precision=highest) + curvature
    scale = jnp.sqrt(squares / population + epsilon)
    return (residue / scale, jnp.concatenate([coefficients, scale[None]]))


def solution(mesh):
    torus = Mesh(
        mesh.devices.reshape(4, 4, 2, mesh.shape["grp"]), ("seg_0", "seg_1", "seg_2", "grp")
    )
    in_specs = (
        P(None, SEG_GRP, None),
        P(SEG_GRP, None, None),
        P(SEG_GRP, None),
        P(SEG_GRP, None, None),
        P(SEG_GRP, None, None),
        P(),
        P(SEG_GRP),
        P(SEG_GRP, None),
        P(SEG_GRP, None),
        P(SEG_GRP, None),
    )
    out_specs = (P(SEG_GRP, None), P())
    return jax.shard_map(
        on_device, mesh=torus, in_specs=in_specs, out_specs=out_specs, check_vma=False
    )
```

profile of v0, /device:TPU:0, one launch (start us, length us, event | category | flops | bytes accessed | tf_op | source)
XLA Modules:
  0.0 194.8 jit_solution(17818676448152926383)
XLA Ops:
  6.1 4.4 %all-to-all-start = ((f32[4,24,761]{2,1,0:T(8,128)}), f32[4,24,761]{2,1,0:T(8,128)S(1)}, u32[]{:S(2)}, u32[]{:S(2)}) async-start(f32[4,24,761]{2,1,0:T(8,128)} %broadcast_in_dim.39), calls=%async_computation | async-start | bytes 589824 | tf_op jit(solution)/shard_map/all_to_all | solution.py:17
  11.1 6.5 %all-to-all-done = f32[4,24,761]{2,1,0:T(8,128)S(1)} async-done(((f32[4,24,761]{2,1,0:T(8,128)}), f32[4,24,761]{2,1,0:T(8,128)S(1)}, u32[]{:S(2)}, u32[]{:S(2)}) %all-to-all-start) | async-done | bytes 292256 | tf_op jit(solution)/shard_map/all_to_all | solution.py:17
  18.9 3.0 %collective-permute-start.2 = (f32[96,121]{1,0:T(8,128)S(1)}, f32[96,121]{1,0:T(8,128)S(1)}, u32[]{:S(2)}, u32[]{:S(2)}) collective-permute-start(f32[96,121]{1,0:T(8,128)S(1)} %split.9), channel_id=1, source_target_pairs={{0,4},{4,8},{8,12},{12,16},{16,20},{20,24},{24,28},{28,32},{32,36}... | collective-permute-start | bytes 139400 | tf_op jit(solution)/shard_map/ppermute | solution.py:51
  25.6 4.8 %collective-permute-start = (f32[96,5,128]{0,2,1:T(8,128)}, f32[96,5,128]{0,2,1:T(8,128)}, u32[]{:S(2)}, u32[]{:S(2)}) collective-permute-start(f32[96,5,128]{0,2,1:T(8,128)} %bitcast.9), channel_id=1, source_target_pairs={{0,4},{4,8},{8,12},{12,16},{16,20},{20,24},{24,28},{28,32},{32,36}... | collective-permute-start | bytes 737288 | tf_op jit(solution)/shard_map/ppermute | solution.py:51
  30.4 7.4 %gather_fusion.1 = f32[4536,121]{1,0:T(8,128)S(1)} fusion(f32[288,121]{1,0:T(8,128)S(1)} %pad_maximum_fusion.1, s32[5120]{0:T(1024)S(1)} %pad_clamp_fusion.1), kind=kCustom, calls=%fused_computation.1 | custom fusion | bytes 4408992 | tf_op jit(solution)/shard_map/jit(_take)/gather | solution.py:86
  39.5 10.6 %fusion.3 = f32[24,316,121]{2,1,0:T(8,128)S(1)} fusion(s32[24,189]{1,0:T(8,128)S(1)} %copy-done.4, f32[24,189,121]{2,1,0:T(8,128)} %reshape.114, pred[24,189]{1,0:T(8,128)(4,1)S(1)} %compare_and_fusion.1), kind=kOutput, calls=%fused_computation.17 | convolution fusion | flops 2083244160 | bytes 5888760 | tf_op jit(solution)/shard_map/tfo,tfk->tok/dot_general | solution.py:90
  50.1 16.4 %fusion.19 = bf16[24,121,1]{1,0,2:T(8,128)(2,1)S(1)} fusion(bf16[316,121,121]{2,0,1:T(8,128)(2,1)} %param.17, f32[24,316,121]{2,1,0:T(8,128)S(1)} %fusion.3), kind=kOutput, calls=%fused_computation.25 | convolution fusion | flops 1332450944 | bytes 12929576 | tf_op jit(solution)/shard_map/tok,oik->ti/dot_general | solution.py:91
  69.0 82.7 %while.11 = (s32[]{:T(128)}, f32[24,128]{1,0:T(8,128)S(1)}, s32[27,24]{1,0:T(8,128)S(1)}, f32[288,5,128]{2,1,0:T(8,128)S(1)}, f32[24,3,128]{2,0,1:T(8,128)S(1)}, /*index=5*/s32[]{:T(128)}, s32[]{:T(128)}) while((s32[]{:T(128)}, f32[24,128]{1,0:T(8,128)S(1)}, s32[27,24]{1,0:T(8,128)S(1)}, f32[288,5,128]{2,1,0:T(8,128)S(1)}, ...), condition=%wide.region_2.3_spmd.clone, body=%wide.region_0.2_spmd.clone.sunk | while | flops 5131483 | bytes 594551 | solution.py:80
  69.8 2.2 %multiply_reduce_fusion.4 = f32[24,128]{1,0:T(8,128)S(1)} fusion(f32[24,128]{1,0:T(8,128)S(1)} %bitcast.99, f32[24,128]{1,0:T(8,128)S(1)} %bitcast.100, f32[24,128]{1,0:T(8,128)S(1)} %get-tuple-element.137, f32[24,128]{1,0:T(8,128)S(1)} %bitcast.101, f32[24,128]{1,0:T(8,128)S(1)} %get-tuple-element.139, f32[24,128]{1,0:T(8,128)S(1)} %bitcast.102, ...), kind=kLoop, calls=%fused_computation.2.clone.1 | loop fusion | flops 5108736 | bytes 110592 | tf_op jit(solution)/shard_map/while/body/eval_jaxpr/reduce_sum | solution.py:78
  72.9 2.2 %multiply_reduce_fusion.4 = f32[24,128]{1,0:T(8,128)S(1)} fusion(f32[24,128]{1,0:T(8,128)S(1)} %bitcast.99, f32[24,128]{1,0:T(8,128)S(1)} %bitcast.100, f32[24,128]{1,0:T(8,128)S(1)} %get-tuple-element.137, f32[24,128]{1,0:T(8,128)S(1)} %bitcast.101, f32[24,128]{1,0:T(8,128)S(1)} %get-tuple-element.139, f32[24,128]{1,0:T(8,128)S(1)} %bitcast.102, ...), kind=kLoop, calls=%fused_computation.2.clone.1 | loop fusion | flops 5108736 | bytes 110592 | tf_op jit(solution)/shard_map/while/body/eval_jaxpr/reduce_sum | solution.py:78
  76.0 2.2 %multiply_reduce_fusion.4 = f32[24,128]{1,0:T(8,128)S(1)} fusion(f32[24,128]{1,0:T(8,128)S(1)} %bitcast.99, f32[24,128]{1,0:T(8,128)S(1)} %bitcast.100, f32[24,128]{1,0:T(8,128)S(1)} %get-tuple-element.137, f32[24,128]{1,0:T(8,128)S(1)} %bitcast.101, f32[24,128]{1,0:T(8,128)S(1)} %get-tuple-element.139, f32[24,128]{1,0:T(8,128)S(1)} %bitcast.102, ...), kind=kLoop, calls=%fused_computation.2.clone.1 | loop fusion | flops 5108736 | bytes 110592 | tf_op jit(solution)/shard_map/while/body/eval_jaxpr/reduce_sum | solution.py:78
  79.0 2.2 %multiply_reduce_fusion.4 = f32[24,128]{1,0:T(8,128)S(1)} fusion(f32[24,128]{1,0:T(8,128)S(1)} %bitcast.99, f32[24,128]{1,0:T(8,128)S(1)} %bitcast.100, f32[24,128]{1,0:T(8,128)S(1)} %get-tuple-element.137, f32[24,128]{1,0:T(8,128)S(1)} %bitcast.101, f32[24,128]{1,0:T(8,128)S(1)} %get-tuple-element.139, f32[24,128]{1,0:T(8,128)S(1)} %bitcast.102, ...), kind=kLoop, calls=%fused_computation.2.clone.1 | loop fusion | flops 5108736 | bytes 110592 | tf_op jit(solution)/shard_map/while/body/eval_jaxpr/reduce_sum | solution.py:78
  82.1 2.2 %multiply_reduce_fusion.4 = f32[24,128]{1,0:T(8,128)S(1)} fusion(f32[24,128]{1,0:T(8,128)S(1)} %bitcast.99, f32[24,128]{1,0:T(8,128)S(1)} %bitcast.100, f32[24,128]{1,0:T(8,128)S(1)} %get-tuple-element.137, f32[24,128]{1,0:T(8,128)S(1)} %bitcast.101, f32[24,128]{1,0:T(8,128)S(1)} %get-tuple-element.139, f32[24,128]{1,0:T(8,128)S(1)} %bitcast.102, ...), kind=kLoop, calls=%fused_computation.2.clone.1 | loop fusion | flops 5108736 | bytes 110592 | tf_op jit(solution)/shard_map/while/body/eval_jaxpr/reduce_sum | solution.py:78
  85.1 2.2 %multiply_reduce_fusion.4 = f32[24,128]{1,0:T(8,128)S(1)} fusion(f32[24,128]{1,0:T(8,128)S(1)} %bitcast.99, f32[24,128]{1,0:T(8,128)S(1)} %bitcast.100, f32[24,128]{1,0:T(8,128)S(1)} %get-tuple-element.137, f32[24,128]{1,0:T(8,128)S(1)} %bitcast.101, f32[24,128]{1,0:T(8,128)S(1)} %get-tuple-element.139, f32[24,128]{1,0:T(8,128)S(1)} %bitcast.102, ...), kind=kLoop, calls=%fused_computation.2.clone.1 | loop fusion | flops 5108736 | bytes 110592 | tf_op jit(solution)/shard_map/while/body/eval_jaxpr/reduce_sum | solution.py:78
  88.2 2.2 %multiply_reduce_fusion.4 = f32[24,128]{1,0:T(8,128)S(1)} fusion(f32[24,128]{1,0:T(8,128)S(1)} %bitcast.99, f32[24,128]{1,0:T(8,128)S(1)} %bitcast.100, f32[24,128]{1,0:T(8,128)S(1)} %get-tuple-element.137, f32[24,128]{1,0:T(8,128)S(1)} %bitcast.101, f32[24,128]{1,0:T(8,128)S(1)} %get-tuple-element.139, f32[24,128]{1,0:T(8,128)S(1)} %bitcast.102, ...), kind=kLoop, calls=%fused_computation.2.clone.1 | loop fusion | flops 5108736 | bytes 110592 | tf_op jit(solution)/shard_map/while/body/eval_jaxpr/reduce_sum | solution.py:78
  91.3 2.2 %multiply_reduce_fusion.4 = f32[24,128]{1,0:T(8,128)S(1)} fusion(f32[24,128]{1,0:T(8,128)S(1)} %bitcast.99, f32[24,128]{1,0:T(8,128)S(1)} %bitcast.100, f32[24,128]{1,0:T(8,128)S(1)} %get-tuple-element.137, f32[24,128]{1,0:T(8,128)S(1)} %bitcast.101, f32[24,128]{1,0:T(8,128)S(1)} %get-tuple-element.139, f32[24,128]{1,0:T(8,128)S(1)} %bitcast.102, ...), kind=kLoop, calls=%fused_computation.2.clone.1 | loop fusion | flops 5108736 | bytes 110592 | tf_op jit(solution)/shard_map/while/body/eval_jaxpr/reduce_sum | solution.py:78
  94.3 2.2 %multiply_reduce_fusion.4 = f32[24,128]{1,0:T(8,128)S(1)} fusion(f32[24,128]{1,0:T(8,128)S(1)} %bitcast.99, f32[24,128]{1,0:T(8,128)S(1)} %bitcast.100, f32[24,128]{1,0:T(8,128)S(1)} %get-tuple-element.137, f32[24,128]{1,0:T(8,128)S(1)} %bitcast.101, f32[24,128]{1,0:T(8,128)S(1)} %get-tuple-element.139, f32[24,128]{1,0:T(8,128)S(1)} %bitcast.102, ...), kind=kLoop, calls=%fused_computation.2.clone.1 | loop fusion | flops 5108736 | bytes 110592 | tf_op jit(solution)/shard_map/while/body/eval_jaxpr/reduce_sum | solution.py:78
  97.4 2.2 %multiply_reduce_fusion.4 = f32[24,128]{1,0:T(8,128)S(1)} fusion(f32[24,128]{1,0:T(8,128)S(1)} %bitcast.99, f32[24,128]{1,0:T(8,128)S(1)} %bitcast.100, f32[24,128]{1,0:T(8,128)S(1)} %get-tuple-element.137, f32[24,128]{1,0:T(8,128)S(1)} %bitcast.101, f32[24,128]{1,0:T(8,128)S(1)} %get-tuple-element.139, f32[24,128]{1,0:T(8,128)S(1)} %bitcast.102, ...), kind=kLoop, calls=%fused_computation.2.clone.1 | loop fusion | flops 5108736 | bytes 110592 | tf_op jit(solution)/shard_map/while/body/eval_jaxpr/reduce_sum | solution.py:78
  100.5 2.2 %multiply_reduce_fusion.4 = f32[24,128]{1,0:T(8,128)S(1)} fusion(f32[24,128]{1,0:T(8,128)S(1)} %bitcast.99, f32[24,128]{1,0:T(8,128)S(1)} %bitcast.100, f32[24,128]{1,0:T(8,128)S(1)} %get-tuple-element.137, f32[24,128]{1,0:T(8,128)S(1)} %bitcast.101, f32[24,128]{1,0:T(8,128)S(1)} %get-tuple-element.139, f32[24,128]{1,0:T(8,128)S(1)} %bitcast.102, ...), kind=kLoop, calls=%fused_computation.2.clone.1 | loop fusion | flops 5108736 | bytes 110592 | tf_op jit(solution)/shard_map/while/body/eval_jaxpr/reduce_sum | solution.py:78
  103.5 2.2 %multiply_reduce_fusion.4 = f32[24,128]{1,0:T(8,128)S(1)} fusion(f32[24,128]{1,0:T(8,128)S(1)} %bitcast.99, f32[24,128]{1,0:T(8,128)S(1)} %bitcast.100, f32[24,128]{1,0:T(8,128)S(1)} %get-tuple-element.137, f32[24,128]{1,0:T(8,128)S(1)} %bitcast.101, f32[24,128]{1,0:T(8,128)S(1)} %get-tuple-element.139, f32[24,128]{1,0:T(8,128)S(1)} %bitcast.102, ...), kind=kLoop, calls=%fused_computation.2.clone.1 | loop fusion | flops 5108736 | bytes 110592 | tf_op jit(solution)/shard_map/while/body/eval_jaxpr/reduce_sum | solution.py:78
  106.6 2.2 %multiply_reduce_fusion.4 = f32[24,128]{1,0:T(8,128)S(1)} fusion(f32[24,128]{1,0:T(8,128)S(1)} %bitcast.99, f32[24,128]{1,0:T(8,128)S(1)} %bitcast.100, f32[24,128]{1,0:T(8,128)S(1)} %get-tuple-element.137, f32[24,128]{1,0:T(8,128)S(1)} %bitcast.101, f32[24,128]{1,0:T(8,128)S(1)} %get-tuple-element.139, f32[24,128]{1,0:T(8,128)S(1)} %bitcast.102, ...), kind=kLoop, calls=%fused_computation.2.clone.1 | loop fusion | flops 5108736 | bytes 110592 | tf_op jit(solution)/shard_map/while/body/eval_jaxpr/reduce_sum | solution.py:78
  109.7 2.2 %multiply_reduce_fusion.4 = f32[24,128]{1,0:T(8,128)S(1)} fusion(f32[24,128]{1,0:T(8,128)S(1)} %bitcast.99, f32[24,128]{1,0:T(8,128)S(1)} %bitcast.100, f32[24,128]{1,0:T(8,128)S(1)} %get-tuple-element.137, f32[24,128]{1,0:T(8,128)S(1)} %bitcast.101, f32[24,128]{1,0:T(8,128)S(1)} %get-tuple-element.139, f32[24,128]{1,0:T(8,128)S(1)} %bitcast.102, ...), kind=kLoop, calls=%fused_computation.2.clone.1 | loop fusion | flops 5108736 | bytes 110592 | tf_op jit(solution)/shard_map/while/body/eval_jaxpr/reduce_sum | solution.py:78
  112.7 2.2 %multiply_reduce_fusion.4 = f32[24,128]{1,0:T(8,128)S(1)} fusion(f32[24,128]{1,0:T(8,128)S(1)} %bitcast.99, f32[24,128]{1,0:T(8,128)S(1)} %bitcast.100, f32[24,128]{1,0:T(8,128)S(1)} %get-tuple-element.137, f32[24,128]{1,0:T(8,128)S(1)} %bitcast.101, f32[24,128]{1,0:T(8,128)S(1)} %get-tuple-element.139, f32[24,128]{1,0:T(8,128)S(1)} %bitcast.102, ...), kind=kLoop, calls=%fused_computation.2.clone.1 | loop fusion | flops 5108736 | bytes 110592 | tf_op jit(solution)/shard_map/while/body/eval_jaxpr/reduce_sum | solution.py:78
  115.8 2.2 %multiply_reduce_fusion.4 = f32[24,128]{1,0:T(8,128)S(1)} fusion(f32[24,128]{1,0:T(8,128)S(1)} %bitcast.99, f32[24,128]{1,0:T(8,128)S(1)} %bitcast.100, f32[24,128]{1,0:T(8,128)S(1)} %get-tuple-element.137, f32[24,128]{1,0:T(8,128)S(1)} %bitcast.101, f32[24,128]{1,0:T(8,128)S(1)} %get-tuple-element.139, f32[24,128]{1,0:T(8,128)S(1)} %bitcast.102, ...), kind=kLoop, calls=%fused_computation.2.clone.1 | loop fusion | flops 5108736 | bytes 110592 | tf_op jit(solution)/shard_map/while/body/eval_jaxpr/reduce_sum | solution.py:78
  118.8 2.2 %multiply_reduce_fusion.4 = f32[24,128]{1,0:T(8,128)S(1)} fusion(f32[24,128]{1,0:T(8,128)S(1)} %bitcast.99, f32[24,128]{1,0:T(8,128)S(1)} %bitcast.100, f32[24,128]{1,0:T(8,128)S(1)} %get-tuple-element.137, f32[24,128]{1,0:T(8,128)S(1)} %bitcast.101, f32[24,128]{1,0:T(8,128)S(1)} %get-tuple-element.139, f32[24,128]{1,0:T(8,128)S(1)} %bitcast.102, ...), kind=kLoop, calls=%fused_computation.2.clone.1 | loop fusion | flops 5108736 | bytes 110592 | tf_op jit(solution)/shard_map/while/body/eval_jaxpr/reduce_sum | solution.py:78
  121.9 2.2 %multiply_reduce_fusion.4 = f32[24,128]{1,0:T(8,128)S(1)} fusion(f32[24,128]{1,0:T(8,128)S(1)} %bitcast.99, f32[24,128]{1,0:T(8,128)S(1)} %bitcast.100, f32[24,128]{1,0:T(8,128)S(1)} %get-tuple-element.137, f32[24,128]{1,0:T(8,128)S(1)} %bitcast.101, f32[24,128]{1,0:T(8,128)S(1)} %get-tuple-element.139, f32[24,128]{1,0:T(8,128)S(1)} %bitcast.102, ...), kind=kLoop, calls=%fused_computation.2.clone.1 | loop fusion | flops 5108736 | bytes 110592 | tf_op jit(solution)/shard_map/while/body/eval_jaxpr/reduce_sum | solution.py:78
  125.0 2.2 %multiply_reduce_fusion.4 = f32[24,128]{1,0:T(8,128)S(1)} fusion(f32[24,128]{1,0:T(8,128)S(1)} %bitcast.99, f32[24,128]{1,0:T(8,128)S(1)} %bitcast.100, f32[24,128]{1,0:T(8,128)S(1)} %get-tuple-element.137, f32[24,128]{1,0:T(8,128)S(1)} %bitcast.101, f32[24,128]{1,0:T(8,128)S(1)} %get-tuple-element.139, f32[24,128]{1,0:T(8,128)S(1)} %bitcast.102, ...), kind=kLoop, calls=%fused_computation.2.clone.1 | loop fusion | flops 5108736 | bytes 110592 | tf_op jit(solution)/shard_map/while/body/eval_jaxpr/reduce_sum | solution.py:78
  128.0 2.2 %multiply_reduce_fusion.4 = f32[24,128]{1,0:T(8,128)S(1)} fusion(f32[24,128]{1,0:T(8,128)S(1)} %bitcast.99, f32[24,128]{1,0:T(8,128)S(1)} %bitcast.100, f32[24,128]{1,0:T(8,128)S(1)} %get-tuple-element.137, f32[24,128]{1,0:T(8,128)S(1)} %bitcast.101, f32[24,128]{1,0:T(8,128)S(1)} %get-tuple-element.139, f32[24,128]{1,0:T(8,128)S(1)} %bitcast.102, ...), kind=kLoop, calls=%fused_computation.2.clone.1 | loop fusion | flops 5108736 | bytes 110592 | tf_op jit(solution)/shard_map/while/body/eval_jaxpr/reduce_sum | solution.py:78
  152.7 14.8 %all-reduce.2 = (f32[8]{0:T(128)S(1)}, f32[]{:T(128)}, f32[]{:T(128)}, f32[8,8]{1,0:T(8,128)S(1)}) all-reduce(f32[8]{0:T(128)S(1)} %convolution_bitcast_fusion.2, f32[]{:T(128)S(6)} %mul.76, f32[]{:T(128)} %get-tuple-element.86, f32[8,8]{1,0:T(8,128)S(1)} %convolution_bitcast_fusion), channel_id=1, replica_groups=mesh['seg_0'=4,'seg_1'=4,'seg_2'=2,'grp'=4] {'seg_0'}, use_global_device_ids=true, to_apply=%region_3.4 | all-reduce | flops 74 | bytes 592 | tf_op jit(solution)/shard_map/psum | solution.py:62
  167.5 8.4 %all-reduce.1 = (f32[8]{0:T(128)S(1)}, f32[]{:T(128)}, f32[]{:T(128)}, f32[8,8]{1,0:T(8,128)S(1)}) all-reduce(f32[8]{0:T(128)S(1)} %get-tuple-element.76, f32[]{:T(128)} %get-tuple-element.77, f32[]{:T(128)} %get-tuple-element.78, f32[8,8]{1,0:T(8,128)S(1)} %get-tuple-element.79), channel_id=1, replica_groups=mesh['seg_0'=4,'seg_1'=4,'seg_2'=2,'grp'=4] {'seg_1'}, use_global_device_ids=true, to_apply=%region_4.5 | all-reduce | flops 74 | bytes 592 | tf_op jit(solution)/shard_map/psum | solution.py:62
  176.0 3.1 %all-reduce.3 = (f32[8]{0:T(128)S(1)}, f32[]{:T(128)}, f32[]{:T(128)}, f32[8,8]{1,0:T(8,128)S(1)}) all-reduce(f32[8]{0:T(128)S(1)} %get-tuple-element.72, f32[]{:T(128)} %get-tuple-element.73, f32[]{:T(128)} %get-tuple-element.74, f32[8,8]{1,0:T(8,128)S(1)} %get-tuple-element.75), channel_id=1, replica_groups=mesh['seg_0'=4,'seg_1'=4,'seg_2'=2,'grp'=4] {'seg_2'}, use_global_device_ids=true, to_apply=%region_5.6 | all-reduce | flops 74 | bytes 592 | tf_op jit(solution)/shard_map/psum | solution.py:62
  179.0 9.6 %all-reduce = (f32[8]{0:T(128)S(1)}, f32[]{:T(128)}, f32[]{:T(128)}, f32[8,8]{1,0:T(8,128)S(1)}) all-reduce(f32[8]{0:T(128)S(1)} %get-tuple-element.80, f32[]{:T(128)} %get-tuple-element.81, f32[]{:T(128)} %get-tuple-element.82, f32[8,8]{1,0:T(8,128)S(1)} %get-tuple-element.83), channel_id=1, replica_groups=mesh['seg_0'=4,'seg_1'=4,'seg_2'=2,'grp'=4] {'grp'}, use_global_device_ids=true, to_apply=%region_6.7 | all-reduce | flops 74 | bytes 592 | tf_op jit(solution)/shard_map/psum | solution.py:62
  (272 shorter events, 54.1 us)
Async XLA Ops:
  0.6 65.9 %copy-start = (bf16[24,128,121]{1,0,2:T(8,128)(2,1)S(1)}, bf16[24,128,121]{1,0,2:T(8,128)(2,1)}, u32[]{:S(2)}) copy-start(bf16[24,128,121]{1,0,2:T(8,128)(2,1)} %param.16) | copy-start | bytes 2230276
  0.6 9.9 %copy-start.2 = (f32[8,24,128]{2,1,0:T(8,128)S(1)}, f32[8,24,128]{2,1,0:T(8,128)}, u32[]{:S(2)}) copy-start(f32[8,24,128]{2,1,0:T(8,128)} %param.12) | copy-start | bytes 294916
  0.7 10.0 %copy-start.3 = (s32[24,189]{1,0:T(8,128)S(1)}, s32[24,189]{1,0:T(8,128)}, u32[]{:S(2)}) copy-start(s32[24,189]{1,0:T(8,128)} %param.20) | copy-start | bytes 54436
  0.7 21.9 %copy-start.5 = (s32[24,27]{1,0:T(8,128)S(1)}, s32[24,27]{1,0:T(8,128)}, u32[]{:S(2)}) copy-start(s32[24,27]{1,0:T(8,128)} %param.19) | copy-start | bytes 7780
  6.1 11.4 %all-to-all-start = ((f32[4,24,761]{2,1,0:T(8,128)}), f32[4,24,761]{2,1,0:T(8,128)S(1)}, u32[]{:S(2)}, u32[]{:S(2)}) async-start(f32[4,24,761]{2,1,0:T(8,128)} %broadcast_in_dim.39), calls=%async_computation | async-start | bytes 589824 | tf_op jit(solution)/shard_map/all_to_all | solution.py:17
  17.6 12.9 %collective-permute-start.3 = (f32[96,121]{1,0:T(8,128)S(1)}, f32[96,121]{1,0:T(8,128)S(1)}, u32[]{:S(2)}, u32[]{:S(2)}) collective-permute-start(f32[96,121]{1,0:T(8,128)S(1)} %split.9), channel_id=1, source_target_pairs={{4,0},{8,4},{12,8},{16,12},{20,16},{24,20},{28,24},{32,28},{36,32}... | collective-permute-start | bytes 139400 | tf_op jit(solution)/shard_map/ppermute | solution.py:53
  18.9 11.6 %collective-permute-start.2 = (f32[96,121]{1,0:T(8,128)S(1)}, f32[96,121]{1,0:T(8,128)S(1)}, u32[]{:S(2)}, u32[]{:S(2)}) collective-permute-start(f32[96,121]{1,0:T(8,128)S(1)} %split.9), channel_id=1, source_target_pairs={{0,4},{4,8},{8,12},{12,16},{16,20},{20,24},{24,28},{28,32},{32,36}... | collective-permute-start | bytes 139400 | tf_op jit(solution)/shard_map/ppermute | solution.py:51
  24.3 42.5 %collective-permute-start.1 = (f32[96,5,128]{0,2,1:T(8,128)}, f32[96,5,128]{0,2,1:T(8,128)}, u32[]{:S(2)}, u32[]{:S(2)}) collective-permute-start(f32[96,5,128]{0,2,1:T(8,128)} %bitcast.9), channel_id=1, source_target_pairs={{4,0},{8,4},{12,8},{16,12},{20,16},{24,20},{28,24},{32,28},{36,32}... | collective-permute-start | bytes 737288 | tf_op jit(solution)/shard_map/ppermute | solution.py:53
  25.6 41.3 %collective-permute-start = (f32[96,5,128]{0,2,1:T(8,128)}, f32[96,5,128]{0,2,1:T(8,128)}, u32[]{:S(2)}, u32[]{:S(2)}) collective-permute-start(f32[96,5,128]{0,2,1:T(8,128)} %bitcast.9), channel_id=1, source_target_pairs={{0,4},{4,8},{8,12},{12,16},{16,20},{20,24},{24,28},{28,32},{32,36}... | collective-permute-start | bytes 737288 | tf_op jit(solution)/shard_map/ppermute | solution.py:51
  37.9 1.6 copy-start.4
  66.8 2.2 %copy-start.1 = (f32[24,3,128]{2,0,1:T(8,128)S(1)}, f32[24,3,128]{2,0,1:T(8,128)}, u32[]{:S(2)}) copy-start(f32[24,3,128]{2,0,1:T(8,128)} %param.13) | copy-start | bytes 110596
where the time goes:
time: 195 us
  other arithmetic  71.5 us (37%)
  blocking collectives  36 us (18%)
  matrix products  30.5 us (16%)
  local copies, waits for them, and re-layouts  28.4 us (15%)
  starting transfers between devices  14.8 us (8%)
  waiting for transfers between devices  6.47 us (3%)
  between operations  4.89 us (3%)
  loops' own time  2.26 us (1%)
    reduce_sum x27, other arithmetic, near_step(): return (running + jnp.sum(kernel * source[:, 4, None, :], axis=2), None)  59.9 us
    psum x4, blocking collectives, by_axis(): value = lax.psum(value, axis)  36 us
    dot_general x1, matrix products, far_field(): jnp.einsum('tok,oik->ti', summed, m2l.astype(jnp.float32), precision=high...  16.4 us
    gather x27, local copies, waits for them, and re-layouts, near_step(): source = jnp.take(wide_panels, column, axis=0)  15.6 us
    dot_general x1, matrix products, far_field(): summed = jnp.einsum('tfo,tfk->tok', offset_hot, gathered, precision=highest)  10.6 us
    gather x2, local copies, waits for them, and re-layouts, far_field(): gathered = jnp.take(wide_poles, far_list, axis=0)  9 us
    ppermute x2, starting transfers between devices, with_halo(): lax.ppermute(tail, axis, [(i, (i + 1) % count) for i in range(ends)])  7.85 us
    all_to_all x1, waiting for transfers between devices, from_everyone(): return lax.all_to_all(copies, axis, split_axis=0, concat_axis=0, tiled=True)  6.46 us
  transfers between devices with their start and end apart: 5, of which 1 were waited for; matrix products, arithmetic and copies ran while one was open for 20% of the time, Pallas kernels for 0%

commit v1 on v0

--- a/solution.py
+++ b/solution.py
@@ -59,7 +59,8 @@
 
 def by_axis(value, axes):
     for axis in axes:
-        value = lax.psum(value, axis)
+        low = lax.all_gather(value, axis_name=axis)
+        value = jnp.sum(low, 0)
     return value
 
 

time: 195 us -> 248 us (1.27)
  blocking collectives: 36 us -> 73 us
  local copies, waits for them, and re-layouts: 28.4 us -> 42.8 us
  waiting for transfers between devices: 6.47 us -> 0.01 us
  other arithmetic: 71.5 us -> 76.2 us
  between operations: 4.89 us -> 7.55 us
    all_gather x0 -> x4, blocking collectives: none -> 40.5 us  [by_axis(): low = lax.all_gather(value, axis_name=axis)]
    psum x4 -> x0, blocking collectives: 36 us -> none  [by_axis(): value = lax.psum(value, axis)]
    unnamed x0 -> x4, blocking collectives: none -> 32.5 us
    unnamed x14 -> x50, local copies, waits for them, and re-layouts: 0.66 us -> 14.7 us
    all_to_all x1, waiting for transfers between devices: 6.46 us -> 0.01 us  [from_everyone(): return lax.all_to_all(copies, axis, split_axis=0, concat_axis=0, tiled=True)]
    reduce_sum x0 -> x15, other arithmetic: none -> 4.89 us  [by_axis(): value = jnp.sum(low, 0)]
  transfers between devices with their start and end apart: 5 -> 5, of which waited for: 1 -> 0; matrix products, arithmetic and copies ran while one was open for 20% -> 17% of each run, Pallas kernels for 0% -> 0%
where the time goes in v1:
time: 248 us; the launch traced here: 247 us
  other arithmetic  76.2 us (31%)
  blocking collectives  73 us (29%)
  local copies, waits for them, and re-layouts  42.8 us (17%)
  matrix products  30.5 us (12%)
  starting transfers between devices  14.5 us (6%)
  between operations  7.55 us (3%)
    reduce_sum x27, other arithmetic, near_step(): return (running + jnp.sum(kernel * source[:, 4, None, :], axis=2), None)  59.9 us
    all_gather x4, blocking collectives, by_axis(): low = lax.all_gather(value, axis_name=axis)  40.5 us
    unnamed x4, blocking collectives  32.5 us
    dot_general x1, matrix products, far_field(): jnp.einsum('tok,oik->ti', summed, m2l.astype(jnp.float32), precision=high...  16.4 us
    gather x27, local copies, waits for them, and re-layouts, near_step(): source = jnp.take(wide_panels, column, axis=0)  15.6 us
    unnamed x50, local copies, waits for them, and re-layouts  14.7 us
    dot_general x1, matrix products, far_field(): summed = jnp.einsum('tfo,tfk->tok', offset_hot, gathered, precision=highest)  10.6 us
    gather x2, local copies, waits for them, and re-layouts, far_field(): gathered = jnp.take(wide_poles, far_list, axis=0)  9 us
  transfers between devices with their start and end apart: 5, of which 0 were waited for; matrix products, arithmetic and copies ran while one was open for 17% of the time, Pallas kernels for 0%

profile of v1, /device:TPU:0, one launch (start us, length us, event | category | flops | bytes accessed | tf_op | source)
XLA Modules:
  0.0 247.0 jit_solution(10930796046966705847)
XLA Ops:
  6.2 4.4 %all-to-all-start = ((f32[4,24,761]{2,1,0:T(8,128)}), f32[4,24,761]{2,1,0:T(8,128)S(1)}, u32[]{:S(2)}, u32[]{:S(2)}) async-start(f32[4,24,761]{2,1,0:T(8,128)} %broadcast_in_dim.39), calls=%async_computation | async-start | bytes 589824 | tf_op jit(solution)/shard_map/all_to_all | solution.py:17
  11.1 12.6 %all-gather.4 = f32[32,8]{1,0:T(8,128)S(1)} all-gather(f32[8,8]{1,0:T(8,128)S(1)} %convolution_bitcast_fusion), channel_id=6, replica_groups=mesh['seg_0'=4,'seg_1'=4,'seg_2'=2,'grp'=4] {'seg_0'}, dimensions={0}, use_global_device_ids=true | all-gather | bytes 1280 | tf_op jit(solution)/shard_map/all_gather | solution.py:62
  23.7 13.2 %all-gather.5 = f32[32,8]{1,0:T(8,128)S(1)} all-gather(f32[8,8]{1,0:T(8,128)S(1)} %bitcast_reduce_fusion.2), channel_id=7, replica_groups=mesh['seg_0'=4,'seg_1'=4,'seg_2'=2,'grp'=4] {'seg_1'}, dimensions={0}, use_global_device_ids=true | all-gather | bytes 1280 | tf_op jit(solution)/shard_map/all_gather | solution.py:62
  38.7 12.9 %all-gather.7 = f32[32,8]{1,0:T(8,128)S(1)} all-gather(f32[8,8]{1,0:T(8,128)S(1)} %bitcast_reduce_fusion.3), channel_id=9, replica_groups=mesh['seg_0'=4,'seg_1'=4,'seg_2'=2,'grp'=4] {'grp'}, dimensions={0}, use_global_device_ids=true | all-gather | bytes 1280 | tf_op jit(solution)/shard_map/all_gather | solution.py:62
  52.9 3.0 %collective-permute-start.2 = (f32[96,121]{1,0:T(8,128)S(1)}, f32[96,121]{1,0:T(8,128)S(1)}, u32[]{:S(2)}, u32[]{:S(2)}) collective-permute-start(f32[96,121]{1,0:T(8,128)S(1)} %split.9), channel_id=1, source_target_pairs={{0,4},{4,8},{8,12},{12,16},{16,20},{20,24},{24,28},{28,32},{32,36}... | collective-permute-start | bytes 139400 | tf_op jit(solution)/shard_map/ppermute | solution.py:51
  65.5 4.5 %collective-permute-start = (f32[96,5,128]{0,2,1:T(8,128)}, f32[96,5,128]{0,2,1:T(8,128)}, u32[]{:S(2)}, u32[]{:S(2)}) collective-permute-start(f32[96,5,128]{0,2,1:T(8,128)} %bitcast.9), channel_id=1, source_target_pairs={{0,4},{4,8},{8,12},{12,16},{16,20},{20,24},{24,28},{28,32},{32,36}... | collective-permute-start | bytes 737288 | tf_op jit(solution)/shard_map/ppermute | solution.py:51
  70.1 7.4 %gather_fusion.1 = f32[4536,121]{1,0:T(8,128)S(1)} fusion(f32[288,121]{1,0:T(8,128)S(1)} %pad_maximum_fusion.1, s32[5120]{0:T(1024)S(1)} %pad_clamp_fusion.1), kind=kCustom, calls=%fused_computation.1 | custom fusion | bytes 4408992 | tf_op jit(solution)/shard_map/jit(_take)/gather | solution.py:87
  79.1 10.6 %fusion.3 = f32[24,316,121]{2,1,0:T(8,128)S(1)} fusion(s32[24,189]{1,0:T(8,128)S(1)} %copy-done.4, f32[24,189,121]{2,1,0:T(8,128)} %reshape.114, pred[24,189]{1,0:T(8,128)(4,1)S(1)} %compare_and_fusion.1), kind=kOutput, calls=%fused_computation.17 | convolution fusion | flops 2083244160 | bytes 5888760 | tf_op jit(solution)/shard_map/tfo,tfk->tok/dot_general | solution.py:91
  89.8 16.4 %fusion.19 = bf16[24,121,1]{1,0,2:T(8,128)(2,1)S(1)} fusion(bf16[316,121,121]{2,0,1:T(8,128)(2,1)} %param.17, f32[24,316,121]{2,1,0:T(8,128)S(1)} %fusion.3), kind=kOutput, calls=%fused_computation.25 | convolution fusion | flops 1332450944 | bytes 12929576 | tf_op jit(solution)/shard_map/tok,oik->ti/dot_general | solution.py:92
  108.7 82.7 %while.11 = (s32[]{:T(128)}, f32[24,128]{1,0:T(8,128)S(1)}, s32[27,24]{1,0:T(8,128)S(1)}, f32[288,5,128]{2,1,0:T(8,128)S(1)}, f32[24,3,128]{2,0,1:T(8,128)S(1)}, /*index=5*/s32[]{:T(128)}, s32[]{:T(128)}) while((s32[]{:T(128)}, f32[24,128]{1,0:T(8,128)S(1)}, s32[27,24]{1,0:T(8,128)S(1)}, f32[288,5,128]{2,1,0:T(8,128)S(1)}, ...), condition=%wide.region_2.3_spmd.clone, body=%wide.region_0.2_spmd.clone.sunk | while | flops 5131483 | bytes 594551 | solution.py:81
  109.5 2.2 multiply_reduce_fusion.4
  112.6 2.2 multiply_reduce_fusion.4
  115.6 2.2 multiply_reduce_fusion.4
  118.7 2.2 multiply_reduce_fusion.4
  121.7 2.2 multiply_reduce_fusion.4
  124.8 2.2 multiply_reduce_fusion.4
  127.9 2.2 multiply_reduce_fusion.4
  130.9 2.2 multiply_reduce_fusion.4
  134.0 2.2 multiply_reduce_fusion.4
  137.1 2.2 multiply_reduce_fusion.4
  140.1 2.2 multiply_reduce_fusion.4
  143.2 2.2 multiply_reduce_fusion.4
  146.3 2.2 multiply_reduce_fusion.4
  149.3 2.2 multiply_reduce_fusion.4
  152.4 2.2 multiply_reduce_fusion.4
  155.4 2.2 multiply_reduce_fusion.4
  158.5 2.2 multiply_reduce_fusion.4
  173.8 2.2 multiply_reduce_fusion.4
  194.2 11.6 %all-reduce.14 = (f32[32]{0:T(128)S(1)}, f32[4]{0:T(128)S(1)}, f32[4]{0:T(128)S(1)}) all-reduce(f32[32]{0:T(128)S(1)} %dynamic-update-slice, f32[4]{0:T(128)S(1)} %dynamic-update-slice.4, f32[4]{0:T(128)S(1)} %dynamic-update-slice.8), channel_id=2, replica_groups=mesh['seg_0'=4,'seg_1'=4,'seg_2'=2,'grp'=4] {'seg_0'}, use_global_device_ids=true, to_apply=%add | all-reduce | flops 40 | bytes 320
  210.0 8.4 %all-reduce.13 = (f32[32]{0:T(128)S(1)}, f32[4]{0:T(128)S(1)}, f32[4]{0:T(128)S(1)}) all-reduce(f32[32]{0:T(128)S(1)} %dynamic-update-slice.1, f32[4]{0:T(128)S(1)} %dynamic-update-slice.5, f32[4]{0:T(128)S(1)} %dynamic-update-slice.9), channel_id=3, replica_groups=mesh['seg_0'=4,'seg_1'=4,'seg_2'=2,'grp'=4] {'seg_1'}, use_global_device_ids=true, to_apply=%add.1 | all-reduce | flops 40 | bytes 320
  222.7 2.4 all-reduce.15
  229.5 10.1 %all-reduce.12 = (f32[32]{0:T(128)S(1)}, f32[4]{0:T(128)S(1)}, f32[4]{0:T(128)S(1)}) all-reduce(f32[32]{0:T(128)S(1)} %dynamic-update-slice.3, f32[4]{0:T(128)S(1)} %dynamic-update-slice.7, f32[4]{0:T(128)S(1)} %dynamic-update-slice.11), channel_id=5, replica_groups=mesh['seg_0'=4,'seg_1'=4,'seg_2'=2,'grp'=4] {'grp'}, use_global_device_ids=true, to_apply=%add.3 | all-reduce | flops 40 | bytes 320
  (332 shorter events, 79.6 us)
Async XLA Ops:
  0.6 105.6 %copy-start = (bf16[24,128,121]{1,0,2:T(8,128)(2,1)S(1)}, bf16[24,128,121]{1,0,2:T(8,128)(2,1)}, u32[]{:S(2)}) copy-start(bf16[24,128,121]{1,0,2:T(8,128)(2,1)} %param.16) | copy-start | bytes 2230276
  0.6 56.1 %copy-start.9 = (u32[128]{0:T(128)S(1)}, u32[128]{0:T(128)}, u32[]{:S(2)}) copy-start(u32[128]{0:T(128)} %constant.80) | copy-start | bytes 1540
  0.7 56.7 %copy-start.8 = (u32[128]{0:T(128)S(1)}, u32[128]{0:T(128)}, u32[]{:S(2)}) copy-start(u32[128]{0:T(128)} %constant.75) | copy-start | bytes 1540
  0.7 58.5 %copy-start.7 = (u32[128]{0:T(128)S(1)}, u32[128]{0:T(128)}, u32[]{:S(2)}) copy-start(u32[128]{0:T(128)} %constant.70) | copy-start | bytes 1540
  0.7 59.7 %copy-start.6 = (u32[128]{0:T(128)S(1)}, u32[128]{0:T(128)}, u32[]{:S(2)}) copy-start(u32[128]{0:T(128)} %constant.65) | copy-start | bytes 1540
  0.7 9.9 %copy-start.2 = (f32[8,24,128]{2,1,0:T(8,128)S(1)}, f32[8,24,128]{2,1,0:T(8,128)}, u32[]{:S(2)}) copy-start(f32[8,24,128]{2,1,0:T(8,128)} %param.12) | copy-start | bytes 294916
  0.7 10.0 %copy-start.3 = (s32[24,189]{1,0:T(8,128)S(1)}, s32[24,189]{1,0:T(8,128)}, u32[]{:S(2)}) copy-start(s32[24,189]{1,0:T(8,128)} %param.20) | copy-start | bytes 54436
  0.7 61.0 %copy-start.5 = (s32[24,27]{1,0:T(8,128)S(1)}, s32[24,27]{1,0:T(8,128)}, u32[]{:S(2)}) copy-start(s32[24,27]{1,0:T(8,128)} %param.19) | copy-start | bytes 7780
  6.2 45.4 %all-to-all-start = ((f32[4,24,761]{2,1,0:T(8,128)}), f32[4,24,761]{2,1,0:T(8,128)S(1)}, u32[]{:S(2)}, u32[]{:S(2)}) async-start(f32[4,24,761]{2,1,0:T(8,128)} %broadcast_in_dim.39), calls=%async_computation | async-start | bytes 589824 | tf_op jit(solution)/shard_map/all_to_all | solution.py:17
  51.6 18.4 %collective-permute-start.3 = (f32[96,121]{1,0:T(8,128)S(1)}, f32[96,121]{1,0:T(8,128)S(1)}, u32[]{:S(2)}, u32[]{:S(2)}) collective-permute-start(f32[96,121]{1,0:T(8,128)S(1)} %split.9), channel_id=1, source_target_pairs={{4,0},{8,4},{12,8},{16,12},{20,16},{24,20},{28,24},{32,28},{36,32}... | collective-permute-start | bytes 139400 | tf_op jit(solution)/shard_map/ppermute | solution.py:53
  52.9 17.1 %collective-permute-start.2 = (f32[96,121]{1,0:T(8,128)S(1)}, f32[96,121]{1,0:T(8,128)S(1)}, u32[]{:S(2)}, u32[]{:S(2)}) collective-permute-start(f32[96,121]{1,0:T(8,128)S(1)} %split.9), channel_id=1, source_target_pairs={{0,4},{4,8},{8,12},{12,16},{16,20},{20,24},{24,28},{28,32},{32,36}... | collective-permute-start | bytes 139400 | tf_op jit(solution)/shard_map/ppermute | solution.py:51
  64.3 42.3 %collective-permute-start.1 = (f32[96,5,128]{0,2,1:T(8,128)}, f32[96,5,128]{0,2,1:T(8,128)}, u32[]{:S(2)}, u32[]{:S(2)}) collective-permute-start(f32[96,5,128]{0,2,1:T(8,128)} %bitcast.9), channel_id=1, source_target_pairs={{4,0},{8,4},{12,8},{16,12},{20,16},{24,20},{28,24},{32,28},{36,32}... | collective-permute-start | bytes 737288 | tf_op jit(solution)/shard_map/ppermute | solution.py:53
  65.5 41.0 %collective-permute-start = (f32[96,5,128]{0,2,1:T(8,128)}, f32[96,5,128]{0,2,1:T(8,128)}, u32[]{:S(2)}, u32[]{:S(2)}) collective-permute-start(f32[96,5,128]{0,2,1:T(8,128)} %bitcast.9), channel_id=1, source_target_pairs={{0,4},{4,8},{8,12},{12,16},{16,20},{20,24},{24,28},{28,32},{32,36}... | collective-permute-start | bytes 737288 | tf_op jit(solution)/shard_map/ppermute | solution.py:51
  77.5 1.6 copy-start.4
  106.5 2.2 copy-start.1
